TPU v7x, 32 devices: a whole 2x2x4 slice. The times are simulated.
32 devices in a mesh: ep: 4 (over z), fsdp: 4 (over x, core), tp: 2 (over y).
Axes of the slice: x: 2, y: 2, z: 4, core: 2. Of those that a mesh axis runs over, the one named last changes fastest.
Arguments:
- out_grad: bfloat16 [2048, 4096], P(('ep', 'fsdp')), may hold values from -1.5 to 1.5
- routes: int32 [2048, 2], P(('ep', 'fsdp')), may hold values from 0 to 3, all different within a row; in each aligned block of 128 rows (0 to 127, 128 to 255, ...) at most 128 rows name the same one
- chosen_logits: float32 [2048, 2], P(('ep', 'fsdp')), may hold values from -4 to 4
- routed_inputs: bfloat16 [4, 4, 4, 128, 4096], P('ep', None, 'fsdp'), may hold values from -6 to 6
- w_gate: bfloat16 [4, 4096, 512], P('ep', 'fsdp', 'tp'), may hold values from -0.09375 to 0.09375
- w_up: bfloat16 [4, 4096, 512], P('ep', 'fsdp', 'tp'), may hold values from -0.09375 to 0.09375
- w_down: bfloat16 [4, 512, 4096], P('ep', 'tp', 'fsdp'), may hold values from -0.25 to 0.25
Outputs:
- input_grad: bfloat16 [2048, 4096], P(('ep', 'fsdp'))
- logit_grad: float32 [2048, 2], P(('ep', 'fsdp'))
- grad_gate: float32 [4, 4096, 512], P('ep', 'fsdp', 'tp')
- grad_up: float32 [4, 4096, 512], P('ep', 'fsdp', 'tp')
- grad_down: float32 [4, 512, 4096], P('ep', 'tp', 'fsdp')
Inputs may be any that keep to these rules, and one draw needn't show every extreme that they name: Each row of routes names 2 different experts. In each token group of 128 consecutive rows no expert is named by more than 128 rows, a bound that some block reaches.
All inputs are finite; a program needn't handle non-finite values.
Results may differ from a plain program's by a relative error of at most 0.015.
Values may be sent and summed in bfloat16 or wider, within the bound.
A program may use at most 128 MiB of HBM per device.

v0:
```python
import jax
import jax.numpy as jnp
from jax import lax
from jax.sharding import PartitionSpec as P


def summed_rows(product, width, axis):
    whole = product(jnp.int32(0), width * lax.axis_size(axis)).astype(jnp.bfloat16)
    return lax.psum_scatter(whole, axis, scatter_dimension=0, tiled=True).astype(jnp.float32)


def slot_places(routes, experts, capacity):
    flat_routes = routes.reshape(-1)
    onehot = (flat_routes[:, None] == jnp.arange(experts, dtype=jnp.int32)[None, :]).astype(
        jnp.int32
    )
    earlier = (jnp.cumsum(onehot, axis=0) - onehot).astype(jnp.int32)
    position = jnp.sum(earlier * onehot, axis=1).astype(jnp.int32)
    return (flat_routes * capacity + position).astype(jnp.int32)


def weighted_rows(grad_rows, gate_probs):
    scaled = gate_probs[:, :, None] * grad_rows.astype(jnp.float32)[:, None, :]
    return scaled.astype(jnp.bfloat16).reshape(-1, grad_rows.shape[1])


def fill_slots(values, slot_index, total_slots):
    row_total = values.shape[0]
    source = jnp.full((total_slots,), row_total, jnp.int32)
    source = source.at[slot_index].set(jnp.arange(row_total, dtype=jnp.int32))
    padded = jnp.concatenate([values, jnp.zeros((1, values.shape[1]), values.dtype)], axis=0)
    return jnp.take(padded, source, axis=0)


def combine(returned, slot_index, tokens, per_token):
    picked = jnp.take(returned, slot_index, axis=0).astype(jnp.float32)
    return jnp.sum(picked.reshape(tokens, per_token, -1), axis=1).astype(jnp.bfloat16)


def transpose_dot(left, right):
    return lax.dot_general(
        left, right, (((0,), (0,)), ((), ())), preferred_element_type=jnp.float32
    )


def contract_last(left, right):
    return lax.dot_general(
        left, right, (((1,), (1,)), ((), ())), preferred_element_type=jnp.float32
    )


def body(out_grad, routes, chosen_logits, routed_inputs, w_gate, w_up, w_down):
    experts = lax.axis_size("ep")
    tp_count = lax.axis_size("tp")
    tokens, model_width = out_grad.shape
    per_token = routes.shape[1]
    capacity = routed_inputs.shape[3]
    gate_probs = jax.nn.softmax(chosen_logits, axis=-1)
    slot_index = slot_places(routes, experts, capacity)
    inputs = routed_inputs.reshape(-1, model_width)
    outgoing = fill_slots(weighted_rows(out_grad, gate_probs), slot_index, experts * capacity)
    arrived = lax.all_to_all(
        outgoing.reshape(experts, capacity, model_width),
        "ep",
        split_axis=0,
        concat_axis=0,
        tiled=True,
    )
    scaled = arrived.reshape(-1, model_width)
    gate_full, up_full, down_full = (
        lax.all_gather(w_gate, "fsdp", axis=1, tiled=True),
        lax.all_gather(w_up, "fsdp", axis=1, tiled=True),
        lax.all_gather(w_down, "fsdp", axis=2, tiled=True),
    )
    gate_full = gate_full[0]
    up_full = up_full[0]
    down_full = down_full[0]
    gate_act = jnp.dot(inputs, gate_full, preferred_element_type=jnp.float32)
    up_act = jnp.dot(inputs, up_full, preferred_element_type=jnp.float32)
    sigmoid_gate = jax.nn.sigmoid(gate_act)
    silu_gate = gate_act * sigmoid_gate
    hidden = (silu_gate * up_act).astype(jnp.bfloat16)
    hidden_grad = contract_last(scaled, down_full)
    products = jnp.sum(hidden_grad * hidden.astype(jnp.float32), axis=1)
    up_grad = (hidden_grad * silu_gate).astype(jnp.bfloat16)
    gate_grad = (
        hidden_grad * up_act * sigmoid_gate * (1.0 + gate_act * (1.0 - sigmoid_gate))
    ).astype(jnp.bfloat16)
    slot_part = contract_last(gate_grad, gate_full) + contract_last(up_grad, up_full)
    pair_grads = jnp.concatenate([gate_grad, up_grad], axis=1)

    def grad_term(first_row, row_count):
        input_cols = lax.dynamic_slice_in_dim(inputs, first_row, row_count, 1)
        scaled_cols = lax.dynamic_slice_in_dim(scaled, first_row, row_count, 1)
        gate_up_part = transpose_dot(input_cols, pair_grads)
        down_part = transpose_dot(scaled_cols, hidden)
        return jnp.concatenate([gate_up_part, down_part], axis=1)

    grad_rows = summed_rows(grad_term, model_width // lax.axis_size("fsdp"), "fsdp")
    hidden_units = hidden.shape[1]
    grad_gate = grad_rows[:, :hidden_units][None]
    grad_up = grad_rows[:, hidden_units : 2 * hidden_units][None]
    grad_down = grad_rows[:, 2 * hidden_units :].T[None]
    narrow = model_width // tp_count
    column_sum = lax.psum_scatter(
        slot_part.astype(jnp.bfloat16), "tp", scatter_dimension=1, tiled=True
    ).astype(jnp.float32)
    product_sum = lax.psum(products.astype(jnp.bfloat16), "tp").astype(jnp.float32)
    leaving = (
        column_sum.astype(jnp.bfloat16).reshape(experts, capacity, narrow),
        product_sum.astype(jnp.bfloat16).reshape(experts, capacity),
    )
    back_rows, back_products = (
        lax.all_to_all(leaving[0], "ep", split_axis=0, concat_axis=0, tiled=True),
        lax.all_to_all(leaving[1], "ep", split_axis=0, concat_axis=0, tiled=True),
    )
    combined = combine(back_rows.reshape(-1, narrow), slot_index, tokens, per_token)
    input_grad = lax.all_gather(combined, "tp", axis=1, tiled=True)
    chosen = (
        jnp.take(back_products.reshape(-1), slot_index)
        .astype(jnp.float32)
        .reshape(tokens, per_token)
    )
    logit_grad = chosen - gate_probs * jnp.sum(chosen, axis=1, keepdims=True)
    return (input_grad, logit_grad, grad_gate, grad_up, grad_down)


def solution(mesh):
    in_specs = (
        P(("ep", "fsdp"), None),
        P(("ep", "fsdp"), None),
        P(("ep", "fsdp"), None),
        P("ep", None, "fsdp", None, None),
        P("ep", "fsdp", "tp"),
        P("ep", "fsdp", "tp"),
        P("ep", "tp", "fsdp"),
    )
    out_specs = (
        P(("ep", "fsdp"), None),
        P(("ep", "fsdp"), None),
        P("ep", "fsdp", "tp"),
        P("ep", "fsdp", "tp"),
        P("ep", "tp", "fsdp"),
    )
    return jax.shard_map(body, mesh=mesh, in_specs=in_specs, out_specs=out_specs, check_vma=False)
```

profile of v0, /device:TPU:0, one launch (start us, length us, event | category | flops | bytes accessed | tf_op | source)
XLA Modules:
  0.0 295.3 jit_solution(5243169975518760738)
XLA Ops:
  16.1 5.3 %mul.79 = f32[128,2,4096]{2,1,0:T(2,128)} broadcast(bf16[128,4096]{1,0:T(8,128)(2,1)} %param.7), dimensions={0,2} | broadcast | bytes 5242880 | tf_op jit(solution)/shard_map/mul | solution.py:23
  21.4 6.1 %mul.80 = f32[256,4096]{1,0:T(8,128)} reshape(f32[128,2,4096]{2,1,0:T(2,128)} %mul.79) | data formatting | bytes 8388608 | tf_op jit(solution)/shard_map/mul | solution.py:23
  27.4 2.7 multiply_convert_fusion
  30.4 4.4 %gather_fusion = bf16[512,4096]{1,0:T(8,128)(2,1)} fusion(bf16[257,4096]{1,0:T(8,128)(2,1)S(1)} %concatenate.10, s32[1024]{0:T(1024)S(1)} %pad_clamp_fusion.1), kind=kCustom, calls=%fused_computation | custom fusion | bytes 8390656 | tf_op jit(solution)/shard_map/jit(_take)/gather | solution.py:32
  34.7 4.6 %broadcast_select_fusion = bf16[4,128,4096]{2,1,0:T(8,128)(2,1)} fusion(bf16[4,128,4096]{2,1,0:T(8,128)(2,1)} %bitcast.67, pred[4,128]{1,0:T(4,128)(4,1)S(1)} %and_bitcast_fusion), kind=kLoop, calls=%fused_computation.10 | loop fusion | flops 2097152 | bytes 8389120 | tf_op jit(solution)/shard_map/jit(_take)/select_n | solution.py:32
  39.3 6.4 %all-to-all-start = ((bf16[4,128,4096]{2,1,0:T(8,128)(2,1)}), bf16[4,128,4096]{2,1,0:T(8,128)(2,1)}, u32[]{:S(2)}, u32[]{:S(2)}) async-start(bf16[4,128,4096]{2,1,0:T(8,128)(2,1)} %broadcast_select_fusion), calls=%async_computation | async-start | bytes 8388608 | tf_op jit(solution)/shard_map/all_to_all | solution.py:62
  46.7 4.2 %fusion.3 = f32[512,256]{0,1:T(8,128)S(1)} fusion(bf16[512,4096]{1,0:T(8,128)(2,1)} %bitcast.74, bf16[1,4096,256]{2,1,0:T(8,128)(2,1)} %all-gather.9.cloned.1.call-done), kind=kOutput, calls=%fused_computation.13 | convolution fusion | flops 1073741824 | bytes 6815744 | tf_op jit(solution)/shard_map/dot_general | solution.py:78
  50.9 8.1 %all-gather.7.cloned.1.call-done = bf16[1,4096,256]{2,1,0:T(8,128)(2,1)} async-done(((bf16[1,1024,256]{2,1,0:T(8,128)(2,1)}), bf16[1,4096,256]{2,1,0:T(8,128)(2,1)}) %all-gather.7.cloned.1.call-update) | async-done | bytes 2097168 | tf_op jit(solution)/shard_map/all_gather | solution.py:72
  59.0 4.2 %fusion.6 = f32[512,256]{0,1:T(8,128)S(1)} fusion(bf16[512,4096]{1,0:T(8,128)(2,1)} %bitcast.75, bf16[1,4096,256]{2,1,0:T(8,128)(2,1)} %all-gather.7.cloned.1.call-done), kind=kOutput, calls=%fused_computation.16 | convolution fusion | flops 1073741824 | bytes 6815744 | tf_op jit(solution)/shard_map/dot_general | solution.py:79
  63.2 20.0 %all-gather.5.cloned.1.call-done = bf16[1,256,4096]{2,1,0:T(8,128)(2,1)} async-done(((bf16[1,256,1024]{2,1,0:T(8,128)(2,1)}), bf16[1,256,4096]{2,1,0:T(8,128)(2,1)}) %all-gather.5.cloned.1.call-update) | async-done | bytes 2097168 | tf_op jit(solution)/shard_map/all_gather | solution.py:73
  83.2 56.0 %all-to-all-done = bf16[4,128,4096]{2,1,0:T(8,128)(2,1)} async-done(((bf16[4,128,4096]{2,1,0:T(8,128)(2,1)}), bf16[4,128,4096]{2,1,0:T(8,128)(2,1)}, u32[]{:S(2)}, u32[]{:S(2)}) %all-to-all-start) | async-done | bytes 4194336 | tf_op jit(solution)/shard_map/all_to_all | solution.py:62
  139.2 4.5 %multiply_reduce_fusion = (bf16[512]{0:T(512)(128)(2,1)S(1)}, bf16[512,256]{0,1:T(8,128)(2,1)S(1)}, bf16[512,256]{0,1:T(8,128)(2,1)S(1)}, bf16[512,256]{0,1:T(8,128)(2,1)S(1)}) fusion(f32[512,256]{0,1:T(8,128)S(1)} %fusion.6, f32[512,256]{0,1:T(8,128)S(1)} %fusion.3, bf16[512,4096]{1,0:T(8,128)(2,1)} %bitcast.6, ...), kind=kOutput, calls=%fused_computation.28 | convolution fusion | flops 1076100608 | bytes 8127488 | tf_op jit(solution)/shard_map/dot_general | solution.py:47
  145.3 3.4 %add_convert_fusion = bf16[512,4096]{1,0:T(8,128)(2,1)} fusion(f32[512,4096]{1,0:T(8,128)S(1)} %fusion.1, bf16[512,256]{0,1:T(8,128)(2,1)S(1)} %get-tuple-element.33, bf16[1,4096,256]{2,1,0:T(8,128)(2,1)S(1)} %copy-done), kind=kOutput, calls=%fused_computation.4 | convolution fusion | flops 1077936128 | bytes 14942208 | tf_op jit(solution)/shard_map/dot_general | solution.py:47
  148.8 3.7 %convolution_convert_fusion.1 = bf16[4096,256]{0,1:T(8,128)(2,1)S(1)} fusion(bf16[512,256]{0,1:T(8,128)(2,1)S(1)} %get-tuple-element.28, bf16[512,4096]{1,0:T(8,128)(2,1)} %bitcast.6), kind=kOutput, calls=%fused_computation.8 | convolution fusion | flops 1074790400 | bytes 6553600 | tf_op jit(solution)/shard_map/dot_general | solution.py:41
  152.5 2.4 fusion
  154.9 3.4 %pad_maximum_fusion = bf16[4096,768]{0,1:T(8,128)(2,1)} fusion(bf16[4096,256]{0,1:T(8,128)(2,1)S(1)} %convolution_convert_fusion.1, bf16[4096,512]{0,1:T(8,128)(2,1)S(1)} %fusion), kind=kLoop, calls=%fused_computation.5 | loop fusion | flops 12582912 | bytes 12582912 | tf_op jit(solution)/shard_map/concatenate | solution.py:97
  158.4 5.1 %psum.7 = bf16[4,1,128]{2,0,1:T(4,128)(2,1)S(1)} all-reduce(bf16[4,1,128]{2,0,1:T(4,128)(2,1)S(1)} %bitcast.73), channel_id=1, replica_groups=mesh['ep'=4,'fsdp'=4,'tp'=2] {'tp'}, use_global_device_ids=true, to_apply=%region_9.10 | all-reduce | flops 512 | bytes 2048 | tf_op jit(solution)/shard_map/psum | solution.py:108
  163.5 8.0 %all_to_all.19 = bf16[4,1,128]{2,1,0:T(2,128)(2,1)S(1)} all-to-all(bf16[4,1,128]{2,1,0:T(2,128)(2,1)S(1)} %copy.46), channel_id=1, replica_groups=mesh['ep'=4,'fsdp'=4,'tp'=2] {'ep'}, dimensions={0} | all-to-all | bytes 2048 | tf_op jit(solution)/shard_map/all_to_all | solution.py:115
  171.5 31.0 %reduce-scatter.3.cloned.1.call-done = bf16[512,2048]{1,0:T(8,128)(2,1)} async-done(((bf16[512,4096]{1,0:T(8,128)(2,1)}), bf16[512,2048]{1,0:T(8,128)(2,1)}) %reduce-scatter.3.cloned.1.call-update) | async-done | bytes 2097168 | tf_op jit(solution)/shard_map/reduce_scatter | solution.py:105
  202.5 4.6 %all-to-all-start.1 = ((bf16[4,128,2048]{2,1,0:T(8,128)(2,1)}), bf16[4,128,2048]{2,1,0:T(8,128)(2,1)S(1)}, u32[]{:S(2)}, u32[]{:S(2)}) async-start(bf16[4,128,2048]{2,1,0:T(8,128)(2,1)} %bitcast.68), calls=%async_computation.2 | async-start | bytes 4194304 | tf_op jit(solution)/shard_map/all_to_all | solution.py:114
  209.7 45.4 %all-to-all-done.1 = bf16[4,128,2048]{2,1,0:T(8,128)(2,1)S(1)} async-done(((bf16[4,128,2048]{2,1,0:T(8,128)(2,1)}), bf16[4,128,2048]{2,1,0:T(8,128)(2,1)S(1)}, u32[]{:S(2)}, u32[]{:S(2)}) %all-to-all-start.1) | async-done | bytes 2097184 | tf_op jit(solution)/shard_map/all_to_all | solution.py:114
  257.2 3.2 %fusion.10 = bf16[128,2048]{1,0:T(8,128)(2,1)} fusion(bf16[128,2,2048]{2,1,0:T(2,128)(2,1)S(1)} %gather.21, pred[128,2]{1,0:T(8,128)(4,1)S(1)} %copy.43), kind=kLoop, calls=%fused_computation.21 | loop fusion | flops 786432 | bytes 1573120 | tf_op jit(solution)/shard_map/reduce_sum | solution.py:37
  268.4 17.7 %all-gather.11.cloned.1.call-done = bf16[128,4096]{1,0:T(8,128)(2,1)} async-done(((bf16[128,2048]{1,0:T(8,128)(2,1)}), bf16[128,4096]{1,0:T(8,128)(2,1)}) %all-gather.11.cloned.1.call-update) | async-done | bytes 1048592 | tf_op jit(solution)/shard_map/all_gather | solution.py:118
  286.1 2.3 copy.53
  (69 shorter events, 24.4 us)
Async XLA Ops:
  7.2 39.5 %all-gather.9.cloned.1.call-start = ((), (), s32[]{:S(2)}) async-start(), calls=%async_computation.7 | async-start | bytes 2621440 | tf_op jit(solution)/shard_map/all_gather | solution.py:71
  7.9 51.1 %all-gather.7.cloned.1.call-start = ((), (), s32[]{:S(2)}) async-start(), calls=%async_computation.6 | async-start | bytes 2621440 | tf_op jit(solution)/shard_map/all_gather | solution.py:72
  39.3 99.9 %all-to-all-start = ((bf16[4,128,4096]{2,1,0:T(8,128)(2,1)}), bf16[4,128,4096]{2,1,0:T(8,128)(2,1)}, u32[]{:S(2)}, u32[]{:S(2)}) async-start(bf16[4,128,4096]{2,1,0:T(8,128)(2,1)} %broadcast_select_fusion), calls=%async_computation | async-start | bytes 8388608 | tf_op jit(solution)/shard_map/all_to_all | solution.py:62
  45.7 37.5 %all-gather.5.cloned.1.call-start = ((), (), s32[]{:S(2)}) async-start(), calls=%async_computation.5 | async-start | bytes 2621440 | tf_op jit(solution)/shard_map/all_gather | solution.py:73
  46.4 156.1 %reduce-scatter.3.cloned.1.call-start = ((), (), s32[]{:S(2)}) async-start(), calls=%async_computation.8 | async-start | bytes 6291456 | tf_op jit(solution)/shard_map/reduce_scatter | solution.py:105
  139.2 4.5 %copy-start.1 = (bf16[1,4096,256]{2,1,0:T(8,128)(2,1)S(1)}, bf16[1,4096,256]{2,1,0:T(8,128)(2,1)}, u32[]{:S(2)}) copy-start(bf16[1,4096,256]{2,1,0:T(8,128)(2,1)} %all-gather.9.cloned.1.call-done) | copy-start | bytes 6291460
  143.7 1.6 copy-start
  148.8 114.1 %reduce-scatter.5.cloned.1.call-start = ((), (), s32[]{:S(2)}) async-start(), calls=%async_computation.10 | async-start | bytes 7864320 | tf_op jit(solution)/shard_map/reduce_scatter | solution.py:9
  148.8 3.7 %copy-start.4 = (bf16[1,4,1,128,4096]{4,3,2,1,0:T(8,128)(2,1)S(1)}, bf16[1,4,1,128,4096]{4,3,2,1,0:T(8,128)(2,1)}, u32[]{:S(2)}) copy-start(bf16[1,4,1,128,4096]{4,3,2,1,0:T(8,128)(2,1)} %param.10) | copy-start | bytes 12582916
  158.3 51.2 %copy-start.3 = (s32[128,2]{0,1:T(2,128)S(1)}, s32[128,2]{0,1:T(2,128)}, u32[]{:S(2)}) copy-start(s32[128,2]{0,1:T(2,128)} %param.8) | copy-start | bytes 3076
  202.5 52.6 %all-to-all-start.1 = ((bf16[4,128,2048]{2,1,0:T(8,128)(2,1)}), bf16[4,128,2048]{2,1,0:T(8,128)(2,1)S(1)}, u32[]{:S(2)}, u32[]{:S(2)}) async-start(bf16[4,128,2048]{2,1,0:T(8,128)(2,1)} %bitcast.68), calls=%async_computation.2 | async-start | bytes 4194304 | tf_op jit(solution)/shard_map/all_to_all | solution.py:114
  207.1 79.0 %all-gather.11.cloned.1.call-start = ((), (), s32[]{:S(2)}) async-start(), calls=%async_computation.9 | async-start | bytes 1572864 | tf_op jit(solution)/shard_map/all_gather | solution.py:118
  256.5 3.9 %copy-start.2 = (f32[128,2]{0,1:T(2,128)S(1)}, f32[128,2]{0,1:T(2,128)}, u32[]{:S(2)}) copy-start(f32[128,2]{0,1:T(2,128)} %param.9) | copy-start | bytes 3076
Sparse Core Ops, SparseCore 0:
  9.5 25.2 all-gather.8
  36.4 22.5 all-gather.6
  60.6 22.5 all-gather.4
  148.9 53.5 reduce-scatter.2
  204.9 57.8 reduce-scatter.4
  264.8 21.2 all-gather.10
where the time goes:
time: 296 us; the launch traced here: 295 us
  waiting for transfers between devices  182 us (61%)
  local copies, waits for them, and re-layouts  30.2 us (10%)
  matrix products  23.6 us (8%)
  other arithmetic  20.4 us (7%)
  between operations  14.3 us (5%)
  blocking collectives  13.1 us (4%)
  starting transfers between devices  11.3 us (4%)
    all_to_all x1, waiting for transfers between devices, body(): lax.all_to_all(outgoing.reshape(experts, capacity, model_width), 'ep', sp...  56 us
    all_to_all x1, waiting for transfers between devices, body(): lax.all_to_all(leaving[0], 'ep', split_axis=0, concat_axis=0, tiled=True)  45.4 us
    reduce_scatter x1, waiting for transfers between devices, body(): lax.psum_scatter(slot_part.astype(jnp.bfloat16), 'tp', scatter_dimension=...  31 us
    all_gather x1, waiting for transfers between devices, body(): lax.all_gather(w_down, 'fsdp', axis=2, tiled=True)  20 us
    all_gather x1, waiting for transfers between devices, body(): input_grad = lax.all_gather(combined, 'tp', axis=1, tiled=True)  17.7 us
    mul x3, local copies, waits for them, and re-layouts, weighted_rows(): scaled = gate_probs[:, :, None] * grad_rows.astype(jnp.float32)[:, None, :]  11.5 us
    dot_general x3, matrix products, contract_last(): lax.dot_general(left, right, (((1,), (1,)), ((), ())), preferred_element_...  9.23 us
    all_gather x1, waiting for transfers between devices, body(): lax.all_gather(w_up, 'fsdp', axis=1, tiled=True)  8.14 us
  transfers between devices with their start and end apart: 8, of which 7 were waited for; matrix products, arithmetic and copies ran while one was open for 21% of the time, Pallas kernels for 0%

commit v1 on v0

--- a/solution.py
+++ b/solution.py
@@ -70,7 +70,9 @@
     gate_full, up_full, down_full = (
         lax.all_gather(w_gate, "fsdp", axis=1, tiled=True),
         lax.all_gather(w_up, "fsdp", axis=1, tiled=True),
-        lax.all_gather(w_down, "fsdp", axis=2, tiled=True),
+        jnp.concatenate(
+            lax.all_to_all(jnp.stack([w_down] * lax.axis_size("fsdp")), "fsdp", 0, 0), axis=2
+        ),
     )
     gate_full = gate_full[0]
     up_full = up_full[0]

time: 296 us -> 307 us (1.037)
  waiting for transfers between devices: 182 us -> 192 us
  starting transfers between devices: 11.3 us -> 15.1 us
    all_gather x1 -> x0, waiting for transfers between devices: 20 us -> none  [body(): lax.all_gather(w_down, 'fsdp', axis=2, tiled=True)]
    all_gather x1, waiting for transfers between devices: 8.14 us -> 20.3 us  [body(): lax.all_gather(w_up, 'fsdp', axis=1, tiled=True)]
    all_to_all x0 -> x1, waiting for transfers between devices: none -> 11.5 us  [body(): lax.all_to_all(jnp.stack([w_down] * lax.axis_size('fsdp')), 'fsdp', 0, 0)]
    all_to_all x1, waiting for transfers between devices: 56 us -> 63.5 us  [body(): lax.all_to_all(outgoing.reshape(experts, capacity, model_width), 'ep', sp...]
    all_to_all x0 -> x1, starting transfers between devices: none -> 4.48 us  [body(): lax.all_to_all(jnp.stack([w_down] * lax.axis_size('fsdp')), 'fsdp', 0, 0)]
  transfers between devices with their start and end apart: 8 -> 8, of which waited for: 7 -> 7; matrix products, arithmetic and copies ran while one was open for 21% -> 20% of each run, Pallas kernels for 0% -> 0%
where the time goes in v1:
time: 307 us
  waiting for transfers between devices  192 us (63%)
  local copies, waits for them, and re-layouts  31.1 us (10%)
  matrix products  23.6 us (8%)
  other arithmetic  17.7 us (6%)
  starting transfers between devices  15.1 us (5%)
  between operations  14 us (5%)
  blocking collectives  13.2 us (4%)
    all_to_all x1, waiting for transfers between devices, body(): lax.all_to_all(outgoing.reshape(experts, capacity, model_width), 'ep', sp...  63.5 us
    all_to_all x1, waiting for transfers between devices, body(): lax.all_to_all(leaving[0], 'ep', split_axis=0, concat_axis=0, tiled=True)  45.4 us
    reduce_scatter x1, waiting for transfers between devices, body(): lax.psum_scatter(slot_part.astype(jnp.bfloat16), 'tp', scatter_dimension=...  30.3 us
    all_gather x1, waiting for transfers between devices, body(): lax.all_gather(w_up, 'fsdp', axis=1, tiled=True)  20.3 us
    all_gather x1, waiting for transfers between devices, body(): input_grad = lax.all_gather(combined, 'tp', axis=1, tiled=True)  17.7 us
    all_to_all x1, waiting for transfers between devices, body(): lax.all_to_all(jnp.stack([w_down] * lax.axis_size('fsdp')), 'fsdp', 0, 0)  11.5 us
    mul x3, local copies, waits for them, and re-layouts, weighted_rows(): scaled = gate_probs[:, :, None] * grad_rows.astype(jnp.float32)[:, None, :]  10.2 us
    dot_general x3, matrix products, contract_last(): lax.dot_general(left, right, (((1,), (1,)), ((), ())), preferred_element_...  9.24 us
  transfers between devices with their start and end apart: 8, of which 7 were waited for; matrix products, arithmetic and copies ran while one was open for 20% of the time, Pallas kernels for 0%

profile of v1, /device:TPU:0, one launch (start us, length us, event | category | flops | bytes accessed | tf_op | source)
XLA Modules:
  0.0 306.7 jit_solution(9915884389368124648)
XLA Ops:
  10.8 4.5 %all-to-all-start.1 = ((bf16[4,1,256,1024]{2,3,1,0:T(8,128)(2,1)}), bf16[4,1,256,1024]{2,3,1,0:T(8,128)(2,1)}, u32[]{:S(2)}, u32[]{:S(2)}) async-start(bf16[4,1,256,1024]{2,3,1,0:T(8,128)(2,1)} %stack.2), calls=%async_computation.1 | async-start | bytes 4194304 | tf_op jit(solution)/shard_map/all_to_all | solution.py:74
  17.9 4.0 %mul.79 = f32[128,2,4096]{2,1,0:T(2,128)} broadcast(bf16[128,4096]{1,0:T(8,128)(2,1)S(1)} %copy-done.2), dimensions={0,2} | broadcast | bytes 5242880 | tf_op jit(solution)/shard_map/mul | solution.py:23
  21.9 6.0 %mul.80 = f32[256,4096]{1,0:T(8,128)} reshape(f32[128,2,4096]{2,1,0:T(2,128)} %mul.79) | data formatting | bytes 8388608 | tf_op jit(solution)/shard_map/mul | solution.py:23
  28.0 2.7 multiply_convert_fusion
  32.4 4.4 %gather_fusion = bf16[512,4096]{1,0:T(8,128)(2,1)} fusion(bf16[257,4096]{1,0:T(8,128)(2,1)S(1)} %concatenate.10, s32[1024]{0:T(1024)S(1)} %pad_clamp_fusion.1), kind=kCustom, calls=%fused_computation | custom fusion | bytes 8390656 | tf_op jit(solution)/shard_map/jit(_take)/gather | solution.py:32
  36.7 4.6 %broadcast_select_fusion = bf16[4,128,4096]{2,1,0:T(8,128)(2,1)} fusion(bf16[4,128,4096]{2,1,0:T(8,128)(2,1)} %bitcast.69, pred[4,128]{1,0:T(4,128)(4,1)S(1)} %and_bitcast_fusion), kind=kLoop, calls=%fused_computation.10 | loop fusion | flops 2097152 | bytes 8389120 | tf_op jit(solution)/shard_map/jit(_take)/select_n | solution.py:32
  41.3 11.5 %all-to-all-done.1 = bf16[4,1,256,1024]{2,3,1,0:T(8,128)(2,1)} async-done(((bf16[4,1,256,1024]{2,3,1,0:T(8,128)(2,1)}), bf16[4,1,256,1024]{2,3,1,0:T(8,128)(2,1)}, u32[]{:S(2)}, u32[]{:S(2)}) %all-to-all-start.1) | async-done | bytes 2097184 | tf_op jit(solution)/shard_map/all_to_all | solution.py:74
  52.9 5.7 %all-to-all-start = ((bf16[4,128,4096]{2,1,0:T(8,128)(2,1)}), bf16[4,128,4096]{2,1,0:T(8,128)(2,1)}, u32[]{:S(2)}, u32[]{:S(2)}) async-start(bf16[4,128,4096]{2,1,0:T(8,128)(2,1)} %broadcast_select_fusion), calls=%async_computation | async-start | bytes 8388608 | tf_op jit(solution)/shard_map/all_to_all | solution.py:62
  59.5 4.2 %fusion.3 = f32[512,256]{0,1:T(8,128)S(1)} fusion(bf16[512,4096]{1,0:T(8,128)(2,1)} %bitcast.77, bf16[1,4096,256]{2,1,0:T(8,128)(2,1)} %all-gather.6.cloned.1.call-done), kind=kOutput, calls=%fused_computation.13 | convolution fusion | flops 1073741824 | bytes 6815744 | tf_op jit(solution)/shard_map/dot_general | solution.py:80
  63.7 20.3 %all-gather.4.cloned.1.call-done = bf16[1,4096,256]{2,1,0:T(8,128)(2,1)} async-done(((bf16[1,1024,256]{2,1,0:T(8,128)(2,1)}), bf16[1,4096,256]{2,1,0:T(8,128)(2,1)}) %all-gather.4.cloned.1.call-update) | async-done | bytes 2097168 | tf_op jit(solution)/shard_map/all_gather | solution.py:72
  84.1 4.2 %fusion.6 = f32[512,256]{0,1:T(8,128)S(1)} fusion(bf16[512,4096]{1,0:T(8,128)(2,1)} %bitcast.78, bf16[1,4096,256]{2,1,0:T(8,128)(2,1)} %all-gather.4.cloned.1.call-done), kind=kOutput, calls=%fused_computation.16 | convolution fusion | flops 1073741824 | bytes 6815744 | tf_op jit(solution)/shard_map/dot_general | solution.py:81
  88.2 63.5 %all-to-all-done = bf16[4,128,4096]{2,1,0:T(8,128)(2,1)} async-done(((bf16[4,128,4096]{2,1,0:T(8,128)(2,1)}), bf16[4,128,4096]{2,1,0:T(8,128)(2,1)}, u32[]{:S(2)}, u32[]{:S(2)}) %all-to-all-start) | async-done | bytes 4194336 | tf_op jit(solution)/shard_map/all_to_all | solution.py:62
  151.7 4.5 %multiply_reduce_fusion = (bf16[512]{0:T(512)(128)(2,1)S(1)}, bf16[512,256]{0,1:T(8,128)(2,1)S(1)}, bf16[512,256]{0,1:T(8,128)(2,1)S(1)}, bf16[512,256]{0,1:T(8,128)(2,1)S(1)}) fusion(f32[512,256]{0,1:T(8,128)S(1)} %fusion.6, f32[512,256]{0,1:T(8,128)S(1)} %fusion.3, bf16[512,4096]{1,0:T(8,128)(2,1)} %bitcast.6, bf16[256,4096]{0,1:T(8,128)(2,1)} %bitcast.10), kind=kOutput, calls=%fused_computation.26 | convolution fusion | flops 1076100608 | bytes 8127488 | tf_op jit(solution)/shard_map/dot_general | solution.py:47
  157.8 3.4 %add_convert_fusion = bf16[512,4096]{1,0:T(8,128)(2,1)} fusion(f32[512,4096]{1,0:T(8,128)S(1)} %fusion.1, bf16[512,256]{0,1:T(8,128)(2,1)S(1)} %get-tuple-element.33, bf16[1,4096,256]{2,1,0:T(8,128)(2,1)S(1)} %copy-done), kind=kOutput, calls=%fused_computation.4 | convolution fusion | flops 1077936128 | bytes 14942208 | tf_op jit(solution)/shard_map/dot_general | solution.py:47
  161.3 3.6 %convolution_convert_fusion.1 = bf16[4096,256]{0,1:T(8,128)(2,1)S(1)} fusion(bf16[512,256]{0,1:T(8,128)(2,1)S(1)} %get-tuple-element.28, bf16[512,4096]{1,0:T(8,128)(2,1)} %bitcast.6), kind=kOutput, calls=%fused_computation.8 | convolution fusion | flops 1074790400 | bytes 6553600 | tf_op jit(solution)/shard_map/dot_general | solution.py:41
  164.9 2.4 fusion
  167.3 3.4 %pad_maximum_fusion = bf16[4096,768]{0,1:T(8,128)(2,1)} fusion(bf16[4096,256]{0,1:T(8,128)(2,1)S(1)} %convolution_convert_fusion.1, bf16[4096,512]{0,1:T(8,128)(2,1)S(1)} %fusion), kind=kLoop, calls=%fused_computation.5 | loop fusion | flops 12582912 | bytes 12582912 | tf_op jit(solution)/shard_map/concatenate | solution.py:99
  170.8 5.1 %psum.7 = bf16[4,1,128]{2,0,1:T(4,128)(2,1)S(1)} all-reduce(bf16[4,1,128]{2,0,1:T(4,128)(2,1)S(1)} %bitcast.76), channel_id=1, replica_groups=mesh['ep'=4,'fsdp'=4,'tp'=2] {'tp'}, use_global_device_ids=true, to_apply=%region_9.10 | all-reduce | flops 512 | bytes 2048 | tf_op jit(solution)/shard_map/psum | solution.py:110
  175.9 8.0 %all_to_all.24 = bf16[4,1,128]{2,1,0:T(2,128)(2,1)S(1)} all-to-all(bf16[4,1,128]{2,1,0:T(2,128)(2,1)S(1)} %copy.51), channel_id=1, replica_groups=mesh['ep'=4,'fsdp'=4,'tp'=2] {'ep'}, dimensions={0} | all-to-all | bytes 2048 | tf_op jit(solution)/shard_map/all_to_all | solution.py:117
  184.0 30.3 %reduce-scatter.3.cloned.1.call-done = bf16[512,2048]{1,0:T(8,128)(2,1)} async-done(((bf16[512,4096]{1,0:T(8,128)(2,1)}), bf16[512,2048]{1,0:T(8,128)(2,1)}) %reduce-scatter.3.cloned.1.call-update) | async-done | bytes 2097168 | tf_op jit(solution)/shard_map/reduce_scatter | solution.py:107
  214.3 4.6 %all-to-all-start.2 = ((bf16[4,128,2048]{2,1,0:T(8,128)(2,1)}), bf16[4,128,2048]{2,1,0:T(8,128)(2,1)S(1)}, u32[]{:S(2)}, u32[]{:S(2)}) async-start(bf16[4,128,2048]{2,1,0:T(8,128)(2,1)} %bitcast.70), calls=%async_computation.3 | async-start | bytes 4194304 | tf_op jit(solution)/shard_map/all_to_all | solution.py:116
  221.5 45.4 %all-to-all-done.2 = bf16[4,128,2048]{2,1,0:T(8,128)(2,1)S(1)} async-done(((bf16[4,128,2048]{2,1,0:T(8,128)(2,1)}), bf16[4,128,2048]{2,1,0:T(8,128)(2,1)S(1)}, u32[]{:S(2)}, u32[]{:S(2)}) %all-to-all-start.2) | async-done | bytes 2097184 | tf_op jit(solution)/shard_map/all_to_all | solution.py:116
  269.0 3.2 %fusion.8 = bf16[128,2048]{1,0:T(8,128)(2,1)} fusion(bf16[128,2,2048]{2,1,0:T(2,128)(2,1)S(1)} %gather.21, pred[128,2]{1,0:T(8,128)(4,1)S(1)} %copy.46), kind=kLoop, calls=%fused_computation.19 | loop fusion | flops 786432 | bytes 1573120 | tf_op jit(solution)/shard_map/reduce_sum | solution.py:37
  280.2 17.7 %all-gather.8.cloned.1.call-done = bf16[128,4096]{1,0:T(8,128)(2,1)} async-done(((bf16[128,2048]{1,0:T(8,128)(2,1)}), bf16[128,4096]{1,0:T(8,128)(2,1)}) %all-gather.8.cloned.1.call-update) | async-done | bytes 1048592 | tf_op jit(solution)/shard_map/all_gather | solution.py:120
  (72 shorter events, 25.4 us)
Async XLA Ops:
  7.2 8.1 %copy-start.4 = (s32[128,2]{0,1:T(2,128)S(1)}, s32[128,2]{0,1:T(2,128)}, u32[]{:S(2)}) copy-start(s32[128,2]{0,1:T(2,128)} %param.8) | copy-start | bytes 3076
  7.2 52.4 %all-gather.6.cloned.1.call-start = ((), (), s32[]{:S(2)}) async-start(), calls=%async_computation.7 | async-start | bytes 2621440 | tf_op jit(solution)/shard_map/all_gather | solution.py:71
  7.9 9.6 %copy-start.3 = (f32[128,2]{0,1:T(2,128)S(1)}, f32[128,2]{0,1:T(2,128)}, u32[]{:S(2)}) copy-start(f32[128,2]{0,1:T(2,128)} %param.9) | copy-start | bytes 3076
  7.9 10.0 %copy-start.2 = (bf16[128,4096]{1,0:T(8,128)(2,1)S(1)}, bf16[128,4096]{1,0:T(8,128)(2,1)}, u32[]{:S(2)}) copy-start(bf16[128,4096]{1,0:T(8,128)(2,1)} %param.7) | copy-start | bytes 3145732
  10.8 42.1 %all-to-all-start.1 = ((bf16[4,1,256,1024]{2,3,1,0:T(8,128)(2,1)}), bf16[4,1,256,1024]{2,3,1,0:T(8,128)(2,1)}, u32[]{:S(2)}, u32[]{:S(2)}) async-start(bf16[4,1,256,1024]{2,3,1,0:T(8,128)(2,1)} %stack.2), calls=%async_computation.1 | async-start | bytes 4194304 | tf_op jit(solution)/shard_map/all_to_all | solution.py:74
  52.9 98.8 %all-to-all-start = ((bf16[4,128,4096]{2,1,0:T(8,128)(2,1)}), bf16[4,128,4096]{2,1,0:T(8,128)(2,1)}, u32[]{:S(2)}, u32[]{:S(2)}) async-start(bf16[4,128,4096]{2,1,0:T(8,128)(2,1)} %broadcast_select_fusion), calls=%async_computation | async-start | bytes 8388608 | tf_op jit(solution)/shard_map/all_to_all | solution.py:62
  58.6 25.5 %all-gather.4.cloned.1.call-start = ((), (), s32[]{:S(2)}) async-start(), calls=%async_computation.6 | async-start | bytes 2621440 | tf_op jit(solution)/shard_map/all_gather | solution.py:72
  59.3 155.0 %reduce-scatter.3.cloned.1.call-start = ((), (), s32[]{:S(2)}) async-start(), calls=%async_computation.8 | async-start | bytes 6291456 | tf_op jit(solution)/shard_map/reduce_scatter | solution.py:107
  151.7 4.5 %copy-start.1 = (bf16[1,4096,256]{2,1,0:T(8,128)(2,1)S(1)}, bf16[1,4096,256]{2,1,0:T(8,128)(2,1)}, u32[]{:S(2)}) copy-start(bf16[1,4096,256]{2,1,0:T(8,128)(2,1)} %all-gather.6.cloned.1.call-done) | copy-start | bytes 6291460
  156.2 1.6 copy-start
  161.2 113.3 %reduce-scatter.5.cloned.1.call-start = ((), (), s32[]{:S(2)}) async-start(), calls=%async_computation.10 | async-start | bytes 7864320 | tf_op jit(solution)/shard_map/reduce_scatter | solution.py:9
  161.3 3.6 %copy-start.5 = (bf16[1,4,1,128,4096]{4,3,2,1,0:T(8,128)(2,1)S(1)}, bf16[1,4,1,128,4096]{4,3,2,1,0:T(8,128)(2,1)}, u32[]{:S(2)}) copy-start(bf16[1,4,1,128,4096]{4,3,2,1,0:T(8,128)(2,1)} %param.10) | copy-start | bytes 12582916
  214.3 52.6 %all-to-all-start.2 = ((bf16[4,128,2048]{2,1,0:T(8,128)(2,1)}), bf16[4,128,2048]{2,1,0:T(8,128)(2,1)S(1)}, u32[]{:S(2)}, u32[]{:S(2)}) async-start(bf16[4,128,2048]{2,1,0:T(8,128)(2,1)} %bitcast.70), calls=%async_computation.3 | async-start | bytes 4194304 | tf_op jit(solution)/shard_map/all_to_all | solution.py:116
  218.9 79.0 %all-gather.8.cloned.1.call-start = ((), (), s32[]{:S(2)}) async-start(), calls=%async_computation.9 | async-start | bytes 1572864 | tf_op jit(solution)/shard_map/all_gather | solution.py:120
Sparse Core Ops, SparseCore 0:
  9.5 36.6 all-gather.5
  60.9 23.0 all-gather.3
  161.4 52.8 reduce-scatter.2
  216.7 57.8 reduce-scatter.4
  276.6 21.2 all-gather.7
